TPU v7x, 256 devices: a whole 4x4x8 slice. The times are simulated.
256 devices in a mesh: row: 32 (over y, z), col: 8 (over x, core).
Axes of the slice: x: 4, y: 4, z: 8, core: 2. Of those that a mesh axis runs over, the one named last changes fastest.
Arguments:
- phase: float32 [512, 1024, 1024], P(None, 'row', 'col'), may hold values from -24 to 24
- pairs: int32 [512, 2], replicated, may hold values from 0 to 127, as said below
Outputs:
- solution: float32 [128, 1024, 1024], P(None, 'row', 'col')
Inputs may be any that keep to these rules, and one draw needn't show every extreme that they name: `pairs`: each row holds two different dates, the earlier one first.
All inputs are finite; a program needn't handle non-finite values.
Results may differ from a plain program's by a relative error of at most 0.00018.
Values sent between devices are 32-bit elements; how exact they have to be, the bound alone decides.
A program may use at most 128 MiB of HBM per device.

v0:
```python
import jax
import jax.numpy as jnp
from jax import lax
from jax.experimental import pallas as pl
from jax.experimental.pallas import tpu as pltpu
from jax.sharding import PartitionSpec as P

ND = 128
LAM2 = 0.8 * 0.8
HALO = 5
PAD = 16
DIST_COL = 8
MESH = pl.DeviceIdType.MESH
F32 = jnp.float32
BF16 = jnp.bfloat16


def split(x):
    hi = x.astype(BF16)
    return hi, (x - hi.astype(F32)).astype(BF16)


def krylov_kernel(
    grid_rows, grid_cols, depth_rows,
    phase_ref, pairs_ref, out_ref,
    ph, z, w1, q1, w2, q2, zt, p1t, p2t, xt, nmat, acc, tot, in1, in2, in3, cmask,
    load_sem, store_sem, halo_send, halo_recv, s1s, s1r, s2s, s2r, s3s, s3r,
):
    rows, cols = ph.shape[0], ph.shape[2]
    wide = cols + 2 * DIST_COL
    row, col = lax.axis_index("row"), lax.axis_index("col")
    y_len = grid_rows // depth_rows
    row_y, row_z = row // depth_rows, lax.rem(row, depth_rows)

    first, last = PAD, PAD + cols
    total_rows = rows + 2 * HALO

    def clear_sides(e, carry):
        z[e, 0:PAD, :] = jnp.zeros((PAD, ND), F32)
        z[e, last:last + PAD, :] = jnp.zeros((PAD, ND), F32)
        return carry

    def clear_ends(e, carry):
        for base in (0, HALO + rows):
            z[base + e, first:last, :] = jnp.zeros((cols, ND), F32)
        return carry

    def load(r):
        return pltpu.make_async_copy(phase_ref.at[:, r, 0, :], ph.at[r], load_sem.at[r])

    order = [0, 1, 2, 3, 4, 5, 26, 27, 28, 29, 30, 31] + list(range(6, 26))
    for r in order:
        load(r).start()

    lax.fori_loop(0, total_rows, clear_sides, 0)
    lax.fori_loop(0, HALO, clear_ends, 0)

    around = [(-1, 0), (1, 0), (0, -1), (0, 1), (-1, -1), (-1, 1), (1, -1), (1, 1)]

    def exists(dr, dc):
        ok = jnp.bool_(True)
        if dr < 0:
            ok = row > 0
        if dr > 0:
            ok = row < grid_rows - 1
        if dc < 0:
            ok = ok & (col > 0)
        if dc > 0:
            ok = ok & (col < grid_cols - 1)
        return ok

    def col_peer(k):
        return (row, lax.rem(col + k, grid_cols))

    def y_peer(k):
        return (lax.rem(row_y + k, y_len) * depth_rows + row_z, col)

    def z_peer(k):
        return (row_y * depth_rows + lax.rem(row_z + k, depth_rows), col)

    groups = [
        (grid_cols, col, col_peer, in1, s1s, s1r),
        (y_len, row_y, y_peer, in2, s2s, s2r),
        (depth_rows, row_z, z_peer, in3, s3s, s3r),
    ]
    barrier = pltpu.get_barrier_semaphore()
    for dr, dc in around:
        @pl.when(exists(dr, dc))
        def _():
            pl.semaphore_signal(barrier, inc=1, device_id=(row + dr, col + dc), device_id_type=MESH)
    for size, _me, peer, _buf, _s, _r in groups:
        for k in range(1, size):
            pl.semaphore_signal(barrier, inc=1, device_id=peer(k), device_id_type=MESH)

    dates = lax.broadcasted_iota(jnp.int32, (ND, pairs_ref.shape[1]), 0)
    later = (dates == pairs_ref[1:2, :]).astype(F32)
    earlier = (dates == pairs_ref[0:1, :]).astype(F32)
    gt = (later - earlier).astype(BF16)
    normal = lax.dot_general(gt, gt, (((1,), (1,)), ((), ())), preferred_element_type=F32)
    eye = (
        lax.broadcasted_iota(jnp.int32, (ND, ND), 0) == lax.broadcasted_iota(jnp.int32, (ND, ND), 1)
    )
    trace = jnp.sum(jnp.where(eye, normal, 0.0), keepdims=True)
    frob = jnp.sum(normal * normal, keepdims=True)
    shift = jnp.floor(frob / trace + 20.0 * LAM2 + 0.5)
    shifted = normal - jnp.where(eye, shift, 0.0)
    n_hi = shifted.astype(BF16)
    n_lo = (shifted - n_hi.astype(F32)).astype(BF16)
    both = jnp.concatenate([n_hi, n_lo], axis=1)
    nmat[...] = jnp.concatenate([both, both], axis=0)

    side = lax.broadcasted_iota(jnp.int32, (wide, ND), 0)
    left_ok = jnp.where(col > 0, 1.0, 0.0)
    right_ok = jnp.where(col < grid_cols - 1, 1.0, 0.0)
    cmask[...] = jnp.where(
        side < DIST_COL, left_ok, jnp.where(side >= DIST_COL + cols, right_ok, 1.0)
    )
    top_ok = jnp.where(row > 0, 1.0, 0.0)
    bottom_ok = jnp.where(row < grid_rows - 1, 1.0, 0.0)
    def make_z(r):
        a_hi, a_lo = split(ph[r])
        b_hi, b_lo = split(ph[r + 1])
        hi = jnp.concatenate([a_hi, b_hi], axis=1)
        lo = jnp.concatenate([a_lo, b_lo], axis=1)
        field = jnp.dot(gt, hi, preferred_element_type=F32) + jnp.dot(gt, lo, preferred_element_type=F32)
        for i in range(2):
            part = field[:, i * cols:(i + 1) * cols]
            zt[r + i] = part
            z[HALO + r + i, first:last, :] = part.T

    def z_rows(lo, hi):
        def step(i, carry):
            r = lo + 2 * i
            load(r).wait()
            load(r + 1).wait()
            make_z(r)
            return carry
        lax.fori_loop(0, (hi - lo) // 2, step, 0)

    z_rows(0, 6)
    z_rows(26, 32)

    n_peers = sum(size - 1 for size, *_ in groups)
    n_around = jnp.int32(0)
    for dr, dc in around:
        n_around = n_around + jnp.where(exists(dr, dc), 1, 0)
    pl.semaphore_wait(barrier, n_around + n_peers)

    edge_c = {-1: first, 1: last - DIST_COL, 0: first}
    size_c = {-1: DIST_COL, 1: DIST_COL, 0: cols}
    land_c = {-1: last, 1: first - DIST_COL, 0: first}
    edge_r = {-1: HALO, 1: rows, 0: HALO}
    land_r = {-1: HALO + rows, 1: 0, 0: HALO}
    size_r = {-1: HALO, 1: HALO, 0: rows}

    def halo(i, dr, dc):
        return pltpu.make_async_remote_copy(
            src_ref=z.at[pl.ds(edge_r[dr], size_r[dr]), pl.ds(edge_c[dc], size_c[dc]), :],
            dst_ref=z.at[pl.ds(land_r[dr], size_r[dr]), pl.ds(land_c[dc], size_c[dc]), :],
            send_sem=halo_send.at[i],
            recv_sem=halo_recv.at[i],
            device_id=(row + dr, col + dc),
            device_id_type=MESH,
        )

    def send(i):
        dr, dc = around[i]
        @pl.when(exists(dr, dc))
        def _():
            halo(i, dr, dc).start()

    def arrived(i):
        dr, dc = around[i]
        @pl.when(exists(-dr, -dc))
        def _():
            halo(i, dr, dc).wait_recv()

    for i in (0, 1, 4, 5, 6, 7):
        send(i)
    z_rows(6, 26)
    for i in (2, 3):
        send(i)

    acc[...] = jnp.zeros_like(acc)
    work = pl.ds(PAD - DIST_COL, wide)
    before = pl.ds(PAD - DIST_COL - 1, wide)
    after = pl.ds(PAD - DIST_COL + 1, wide)

    def lap(buf, e):
        beside = buf[e - 1, work, :] + buf[e + 1, work, :] + buf[e, before, :] + buf[e, after, :]
        return 4.0 * buf[e, work, :] - beside

    def row_mask(e):
        return jnp.where(e < HALO, top_ok, jnp.where(e >= HALO + rows, bottom_ok, 1.0))

    def normal_times(value):
        hi, lo = split(value)
        both = jnp.dot(jnp.concatenate([hi, lo], axis=1), nmat[...], preferred_element_type=F32)
        return both[:, :ND] + both[:, ND:]

    def add_to(j, value):
        own = value[DIST_COL:DIST_COL + cols, :]
        acc[j] += jnp.sum(own.reshape(cols // 8, 8, ND), axis=0)

    def each(lo, hi, body):
        def step(e, carry):
            body(e)
            return carry
        lax.fori_loop(lo, hi, step, 0)

    def lap_rows(src, dst, lo, hi):
        def body(e):
            dst[e, work, :] = lap(src, e) * (cmask[...] * row_mask(e))
        each(lo, hi, body)

    def k_rows(src, lap_buf, dst, lo, hi, moments):
        def body(e):
            value = src[e, work, :]
            result = (normal_times(value) + LAM2 * lap(lap_buf, e)) * (cmask[...] * row_mask(e))
            dst[e, work, :] = result
            if moments is not None:
                if moments == 1:
                    add_to(0, value * value)
                add_to(moments, value * result)
                add_to(moments + 1, result * result)
        each(lo, hi, body)

    def last_rows(lo, hi):
        def body(e):
            value = q2[e, work, :]
            bent = lap(q2, e)
            add_to(5, value * normal_times(value) + LAM2 * (bent * bent))
        each(lo, hi, body)

    for i in (2, 3):
        arrived(i)
    lap_rows(z, w1, 6, 36)
    k_rows(z, w1, q1, 7, 35, 1)
    lap_rows(q1, w2, 8, 34)
    k_rows(q1, w2, q2, 9, 33, 3)
    last_rows(10, 32)

    for i in (0, 1, 4, 5, 6, 7):
        arrived(i)
    for lo, hi in ((1, 6), (36, 41)):
        lap_rows(z, w1, lo, hi)
    k_rows(z, w1, q1, 2, 5, None)
    k_rows(z, w1, q1, 5, 7, 1)
    k_rows(z, w1, q1, 35, 37, 1)
    k_rows(z, w1, q1, 37, 40, None)
    for lo, hi in ((3, 8), (34, 39)):
        lap_rows(q1, w2, lo, hi)
    k_rows(q1, w2, q2, 4, 5, None)
    k_rows(q1, w2, q2, 5, 9, 3)
    k_rows(q1, w2, q2, 33, 37, 3)
    k_rows(q1, w2, q2, 37, 38, None)
    last_rows(5, 10)
    last_rows(32, 37)

    tot[0] = jnp.concatenate([jnp.sum(acc[j], axis=0, keepdims=True) for j in range(8)], axis=0)

    def group_copy(stage, k):
        size, me, peer, buf, s_sem, r_sem = groups[stage]
        return pltpu.make_async_remote_copy(
            src_ref=tot.at[stage],
            dst_ref=buf.at[k],
            send_sem=s_sem.at[k],
            recv_sem=r_sem.at[k],
            device_id=peer(k),
            device_id_type=MESH,
        )

    def flip(r, carry):
        p1t[r] = q1[HALO + r, first:last, :].T
        p2t[r] = q2[HALO + r, first:last, :].T
        return carry

    for stage in range(3):
        size = groups[stage][0]
        for k in range(1, size):
            group_copy(stage, k).start()
        if stage == 0:
            lax.fori_loop(0, rows, flip, 0)
        part = tot[stage]
        for k in range(1, size):
            group_copy(stage, k).wait_recv()
        for k in range(1, size):
            part = part + groups[stage][3][k]
        tot[stage + 1] = part

    mu = []
    for j in range(6):
        mu.append(jnp.broadcast_to(jnp.sum(tot[3, j:j + 1, :], axis=1, keepdims=True), (1, ND)))
    s = jnp.broadcast_to(shift, (1, ND))
    h00 = mu[1] + s * mu[0]
    h01 = mu[2] + s * mu[1]
    h02 = mu[3] + s * mu[2]
    h11 = h02
    h12 = mu[4] + s * mu[3]
    h22 = mu[5] + s * mu[4]
    l10, l20 = h01 / h00, h02 / h00
    d1 = h11 - l10 * h01
    e1 = h12 - l20 * h01
    l21 = e1 / d1
    d2 = h22 - l20 * h02 - l21 * e1
    y1 = mu[1] - l10 * mu[0]
    y2 = mu[2] - l20 * mu[0] - l21 * y1
    c2 = y2 / d2
    c1 = y1 / d1 - l21 * c2
    c0 = mu[0] / h00 - l10 * c1 - l20 * c2

    def store(r):
        return pltpu.make_async_copy(xt.at[r], out_ref.at[:, r, 0, :], store_sem.at[r])

    def combine(r, carry):
        xt[r] = c0 * zt[r] + c1 * p1t[r] + c2 * p2t[r]
        store(r).start()
        return carry
    lax.fori_loop(0, rows, combine, 0)

    for i, (dr, dc) in enumerate(around):
        @pl.when(exists(dr, dc))
        def _():
            halo(i, dr, dc).wait_send()
    for stage in range(3):
        for k in range(1, groups[stage][0]):
            group_copy(stage, k).wait_send()

    def finish(r, carry):
        store(r).wait()
        return carry
    lax.fori_loop(0, rows, finish, 0)


def on_device(grid_rows, grid_cols, depth_rows, phase, pairs):
    m, rows, cols = phase.shape
    total_rows, total_cols = rows + 2 * HALO, cols + 2 * PAD
    y_len = grid_rows // depth_rows
    field = pltpu.VMEM((total_rows, total_cols, ND), F32)
    flat = pltpu.VMEM((rows, ND, cols), F32)
    dma = pltpu.SemaphoreType.DMA
    out = pl.pallas_call(
        lambda *refs: krylov_kernel(grid_rows, grid_cols, depth_rows, *refs),
        name="krylov",
        out_shape=jax.ShapeDtypeStruct((ND, rows, 1, cols), F32),
        in_specs=[pl.BlockSpec(memory_space=pltpu.HBM), pl.BlockSpec(memory_space=pltpu.VMEM)],
        out_specs=pl.BlockSpec(memory_space=pltpu.HBM),
        scratch_shapes=[
            pltpu.VMEM((rows, m, cols), F32),
            field, field, field, field, field,
            flat, flat, flat, flat,
            pltpu.VMEM((2 * ND, 2 * ND), BF16),
            pltpu.VMEM((8, 8, ND), F32),
            pltpu.VMEM((4, 8, ND), F32),
            pltpu.VMEM((grid_cols, 8, ND), F32),
            pltpu.VMEM((y_len, 8, ND), F32),
            pltpu.VMEM((depth_rows, 8, ND), F32),
            pltpu.VMEM((cols + 2 * DIST_COL, ND), F32),
            dma((rows,)), dma((rows,)),
            dma((8,)), dma((8,)),
            dma((grid_cols,)), dma((grid_cols,)),
            dma((y_len,)), dma((y_len,)),
            dma((depth_rows,)), dma((depth_rows,)),
        ],
        compiler_params=pltpu.CompilerParams(
            collective_id=0, has_side_effects=True, vmem_limit_bytes=56 * 1024 * 1024
        ),
    )(phase.reshape(m, rows, 1, cols), pairs.T)
    return out.reshape(ND, rows, cols)


def solution(mesh, depth=8):
    grid_rows, grid_cols = mesh.shape["row"], mesh.shape["col"]

    def body(phase, pairs):
        return on_device(grid_rows, grid_cols, depth, phase, pairs)

    return jax.shard_map(
        body,
        mesh=mesh,
        in_specs=(P(None, "row", "col"), P()),
        out_specs=P(None, "row", "col"),
        check_vma=False,
    )
```

profile of v0, /device:TPU:1, one launch (start us, length us, event | category | flops | bytes accessed | tf_op | source)
XLA Modules:
  0.0 55.7 jit_solution(9573958314907495462)
XLA Ops:
  0.0 52.6 %krylov.1 = f32[128,32,1,128]{3,2,1,0:T(1,128)} custom-call(f32[512,32,1,128]{3,2,1,0:T(1,128)} %bitcast.4, s32[2,512]{1,0:T(2,128)} %bitcast.5), custom_call_target="tpu_custom_call" | custom-call | tf_op jit(solution)/shard_map/krylov/pallas_call | solution.py:342
  52.6 3.1 %copy.4 = f32[128,32,128]{2,1,0:T(8,128)} copy(f32[128,32,128]{2,1,0:T(8,128)} %bitcast.3) | data formatting | bytes 4194304
where the time goes:
time: 55.8 us; the launch traced here: 55.7 us
  Pallas kernels  52.6 us (94%)
  local copies, waits for them, and re-layouts  3.08 us (6%)
    pallas_call x1, Pallas kernels, on_device(): pl.pallas_call(lambda *refs: krylov_kernel(grid_rows, grid_cols, depth_ro...  52.6 us
    unnamed x1, local copies, waits for them, and re-layouts  3.08 us

commit v1 on v0

v1 whole, which is shorter than its diff:
```python
import jax
import jax.numpy as jnp
from jax import lax
from jax.experimental import pallas as pl
from jax.experimental.pallas import tpu as pltpu
from jax.sharding import PartitionSpec as P

ND = 128
LAM2 = 0.8 * 0.8
HALO = 5
PAD = 16
DIST_COL = 8
MESH = pl.DeviceIdType.MESH
F32 = jnp.float32
BF16 = jnp.bfloat16


def split(x, terms):
    parts = []
    for _ in range(terms - 1):
        parts.append(x.astype(BF16))
        x = x - parts[-1].astype(F32)
    return parts + [x.astype(BF16)]


def krylov_kernel(
    grid_rows, grid_cols, depth_rows,
    phase_ref, pairs_hbm, zt, p1t, p2t, weights,
    pairs_ref, ph, z, w1, q1, w2, q2, nmat, acc, tot, in1, in2, cmask,
    pairs_sem, load_sem, halo_send, halo_recv, s1s, s1r, s2s, s2r,
):
    rows, cols = ph.shape[0], ph.shape[2]
    wide = cols + 2 * DIST_COL
    row, col = lax.axis_index("row"), lax.axis_index("col")
    y_len = grid_rows // depth_rows
    row_y, row_z = row // depth_rows, lax.rem(row, depth_rows)

    first, last = PAD, PAD + cols
    total_rows = rows + 2 * HALO

    def clear_sides(e, carry):
        z[e, first - DIST_COL:first, :] = jnp.zeros((DIST_COL, ND), F32)
        z[e, last:last + DIST_COL, :] = jnp.zeros((DIST_COL, ND), F32)
        return carry

    def clear_ends(e, carry):
        for base in (0, HALO + rows):
            z[base + e, first:last, :] = jnp.zeros((cols, ND), F32)
        return carry

    def load(r):
        return pltpu.make_async_copy(phase_ref.at[:, r, 0, :], ph.at[r], load_sem.at[r])

    load_pairs = pltpu.make_async_copy(pairs_hbm, pairs_ref, pairs_sem)
    load_pairs.start()
    strips = [0, rows - 8] + list(range(8, rows - 8, 8))
    for r in range(4):
        load(r).start()

    lax.fori_loop(0, total_rows, clear_sides, 0)
    lax.fori_loop(0, HALO, clear_ends, 0)

    around = [(-1, 0), (1, 0), (0, -1), (0, 1), (-1, -1), (-1, 1), (1, -1), (1, 1)]

    def exists(dr, dc):
        ok = jnp.bool_(True)
        if dr < 0:
            ok = row > 0
        if dr > 0:
            ok = row < grid_rows - 1
        if dc < 0:
            ok = ok & (col > 0)
        if dc > 0:
            ok = ok & (col < grid_cols - 1)
        return ok

    def plane_peer(k):
        other_y = lax.rem(row_y + k // grid_cols, y_len)
        return (other_y * depth_rows + row_z, lax.rem(col + k % grid_cols, grid_cols))

    def z_peer(k):
        return (row_y * depth_rows + lax.rem(row_z + k, depth_rows), col)

    groups = [
        (y_len * grid_cols, plane_peer, in1, s1s, s1r),
        (depth_rows, z_peer, in2, s2s, s2r),
    ]
    barrier = pltpu.get_barrier_semaphore()
    for dr, dc in around:
        @pl.when(exists(dr, dc))
        def _():
            pl.semaphore_signal(barrier, inc=1, device_id=(row + dr, col + dc), device_id_type=MESH)
    for size, peer, _buf, _s, _r in groups:
        for k in range(1, size):
            pl.semaphore_signal(barrier, inc=1, device_id=peer(k), device_id_type=MESH)

    load_pairs.wait()
    for base in strips:
        for r in range(max(base, 4), base + 8):
            load(r).start()
    dates = lax.broadcasted_iota(jnp.int32, (ND, pairs_ref.shape[1]), 0)
    later = (dates == pairs_ref[1:2, :]).astype(F32)
    earlier = (dates == pairs_ref[0:1, :]).astype(F32)
    gt = (later - earlier).astype(BF16)
    normal = lax.dot_general(gt, gt, (((1,), (1,)), ((), ())), preferred_element_type=F32)
    eye = (
        lax.broadcasted_iota(jnp.int32, (ND, ND), 0) == lax.broadcasted_iota(jnp.int32, (ND, ND), 1)
    )
    trace = jnp.sum(jnp.where(eye, normal, 0.0), keepdims=True)
    frob = jnp.sum(normal * normal, keepdims=True)
    shift = jnp.floor(frob / trace + 20.0 * LAM2 + 0.5)
    shifted = normal - jnp.where(eye, shift, 0.0)
    n_hi = shifted.astype(BF16)
    n_lo = (shifted - n_hi.astype(F32)).astype(BF16)
    nmat[...] = jnp.concatenate([n_hi, n_hi, n_hi, n_lo], axis=0)

    side = lax.broadcasted_iota(jnp.int32, (wide, ND), 0)
    left_ok = jnp.where(col > 0, 1.0, 0.0)
    right_ok = jnp.where(col < grid_cols - 1, 1.0, 0.0)
    cmask[...] = jnp.where(
        side < DIST_COL, left_ok, jnp.where(side >= DIST_COL + cols, right_ok, 1.0)
    )
    top_ok = jnp.where(row > 0, 1.0, 0.0)
    bottom_ok = jnp.where(row < grid_rows - 1, 1.0, 0.0)
    def make_z(r):
        parts = []
        for j in range(8):
            load(r + j).wait()
            parts.append(split(ph[r + j], 2))
        for half in (parts[:4], parts[4:]):
            field = sum(
                jnp.dot(gt, jnp.concatenate([p[t] for p in half], axis=1), preferred_element_type=F32)
                for t in range(2)
            )
            for j in range(4):
                part = field[:, j * cols:(j + 1) * cols]
                zt[r + j] = part
                z[HALO + r + j, first:last, :] = part.T
            r = r + 4

    top, low = HALO, rows
    pieces = [(-1, 0, top, HALO + rows, HALO), (1, 0, low, 0, HALO)]
    for dc in (-1, 1):
        pieces += [(-1, dc, top, HALO + rows, HALO - 1), (1, dc, low + 1, 1, HALO - 1)]
    for r in strips:
        pieces += [(0, dc, HALO + r, HALO + r, 8) for dc in (-1, 1)]
    edge_c = {-1: first, 1: last - DIST_COL, 0: first}
    size_c = {-1: DIST_COL, 1: DIST_COL, 0: cols}
    land_c = {-1: last, 1: first - DIST_COL, 0: first}

    def halo(i):
        dr, dc, source, target, count = pieces[i]
        return pltpu.make_async_remote_copy(
            src_ref=z.at[pl.ds(source, count), pl.ds(edge_c[dc], size_c[dc]), :],
            dst_ref=z.at[pl.ds(target, count), pl.ds(land_c[dc], size_c[dc]), :],
            send_sem=halo_send.at[i],
            recv_sem=halo_recv.at[i],
            device_id=(row + dr, col + dc),
            device_id_type=MESH,
        )

    def send(i):
        @pl.when(exists(*pieces[i][:2]))
        def _():
            halo(i).start()

    def arrived(i):
        dr, dc = pieces[i][:2]
        @pl.when(exists(-dr, -dc))
        def _():
            halo(i).wait_recv()

    def sent(i):
        @pl.when(exists(*pieces[i][:2]))
        def _():
            halo(i).wait_send()

    for r in strips[:2]:
        make_z(r)
    n_peers = sum(size - 1 for size, *_ in groups)
    n_around = jnp.int32(0)
    for dr, dc in around:
        n_around = n_around + jnp.where(exists(dr, dc), 1, 0)
    pl.semaphore_wait(barrier, n_around + n_peers)
    for i in range(10):
        send(i)
    for part, r in enumerate(strips[2:]):
        make_z(r)
        for i in (10 + 2 * part, 11 + 2 * part):
            send(i)

    acc[...] = jnp.zeros_like(acc)
    work = pl.ds(PAD - DIST_COL, wide)
    before = pl.ds(PAD - DIST_COL - 1, wide)
    after = pl.ds(PAD - DIST_COL + 1, wide)

    def lap(buf, e):
        beside = buf[e - 1, work, :] + buf[e + 1, work, :] + buf[e, before, :] + buf[e, after, :]
        return 4.0 * buf[e, work, :] - beside

    def normal_times(values):
        pieces = []
        for value in values:
            hi, mid, lo = split(value, 3)
            pieces.append(jnp.concatenate([hi, mid, lo, hi], axis=1))
        height = values[0].shape[0]
        half = (len(values) + 1) // 2
        products = []
        for some in (pieces[:half], pieces[half:]):
            both = jnp.dot(jnp.concatenate(some, axis=0), nmat[...], preferred_element_type=F32)
            products += [both[i * height:(i + 1) * height, :] for i in range(len(some))]
        return products

    def own(value):
        return value[DIST_COL:DIST_COL + cols, :]

    def folded(value):
        return jnp.sum(value.reshape(cols // 8, 8, ND), axis=0)

    def masked(value, scale):
        if scale is None:
            ends = (value[:DIST_COL] * cmask[:DIST_COL], value[-DIST_COL:] * cmask[-DIST_COL:])
            return jnp.concatenate([ends[0], own(value), ends[1]], axis=0)
        return value * (cmask[...] * scale)

    def blocks(lo, hi, block, body):
        if hi - lo == block:
            body(lo)
            return

        def step(i, carry):
            body(lo + block * i)
            return carry
        lax.fori_loop(0, (hi - lo) // block, step, 0)

    def scale_of(e):
        if isinstance(e, int):
            return top_ok if e < HALO else bottom_ok if e >= HALO + rows else None
        return None

    def counts(e):
        return not isinstance(e, int) or HALO <= e < HALO + rows

    def lap_rows(src, dst, lo, hi, block):
        def body(base):
            for e in [base + i for i in range(block)]:
                dst[e, work, :] = masked(lap(src, e), scale_of(e))
        blocks(lo, hi, block, body)

    def k_rows(src, lap_buf, dst, flat, lo, hi, block, moment):
        def body(base):
            es = [base + i for i in range(block)]
            sums = [jnp.zeros((8, ND), F32)] * 3
            products = normal_times([src[e, work, :] for e in es])
            for e, product in zip(es, products):
                value = src[e, work, :]
                result = masked(product + LAM2 * lap(lap_buf, e), scale_of(e))
                dst[e, work, :] = result
                if counts(e):
                    mine, new = own(value), own(result)
                    flat[e - HALO] = new.T
                    if moment == 1:
                        sums[0] = sums[0] + folded(mine * mine)
                    sums[1] = sums[1] + folded(mine * new)
                    sums[2] = sums[2] + folded(new * new)
            if moment == 1:
                acc[0] += sums[0]
            acc[moment] += sums[1]
            acc[moment + 1] += sums[2]
        blocks(lo, hi, block, body)

    def last_rows(lo, hi, block):
        def body(base):
            es = [base + i for i in range(block)]
            products = normal_times([q2[e, first:last, :] for e in es])
            total = jnp.zeros((8, ND), F32)
            for e, product in zip(es, products):
                bent = own(lap(q2, e))
                total = total + folded(q2[e, first:last, :] * product + LAM2 * (bent * bent))
            acc[5] += total
        blocks(lo, hi, block, body)

    for i in range(6, len(pieces)):
        arrived(i)
    lap_rows(z, w1, 6, 36, 3)
    k_rows(z, w1, q1, p1t, 7, 35, 7, 1)
    lap_rows(q1, w2, 8, 34, 2)
    k_rows(q1, w2, q2, p2t, 9, 33, 8, 3)
    last_rows(10, 32, 11)

    for i in range(6):
        arrived(i)
    for lo in (1, 36):
        lap_rows(z, w1, lo, lo + 5, 5)
    for lo in (2, 35):
        k_rows(z, w1, q1, p1t, lo, lo + 5, 5, 1)
    for lo in (3, 34):
        lap_rows(q1, w2, lo, lo + 5, 5)
    for lo in (4, 33):
        k_rows(q1, w2, q2, p2t, lo, lo + 5, 5, 3)
    for lo in (5, 32):
        last_rows(lo, lo + 5, 5)

    lines = jnp.concatenate([jnp.sum(acc[j], axis=0, keepdims=True) for j in range(8)], axis=0)
    lines = jnp.broadcast_to(jnp.sum(lines, axis=1, keepdims=True), (8, ND))
    at = lax.broadcasted_iota(jnp.int32, (8, ND), 0) == lax.broadcasted_iota(jnp.int32, (8, ND), 1)
    tot[0] = jnp.sum(jnp.where(at, lines, 0.0), axis=0, keepdims=True)

    def group_copy(stage, k):
        size, peer, buf, s_sem, r_sem = groups[stage]
        return pltpu.make_async_remote_copy(
            src_ref=tot.at[stage],
            dst_ref=buf.at[k],
            send_sem=s_sem.at[k],
            recv_sem=r_sem.at[k],
            device_id=peer(k),
            device_id_type=MESH,
        )

    for stage in range(2):
        size = groups[stage][0]
        for k in range(1, size):
            group_copy(stage, k).start()
        for k in range(1, size):
            group_copy(stage, k).wait_recv()
        part = tot[stage]
        for k in range(1, size):
            part = part + groups[stage][2][k]
        tot[stage + 1] = part

    lane = lax.broadcasted_iota(jnp.int32, (1, ND), 1)
    mu = []
    for j in range(6):
        mu.append(jnp.broadcast_to(jnp.sum(jnp.where(lane == j, tot[2], 0.0), axis=1, keepdims=True), (1, ND)))
    s = jnp.broadcast_to(shift, (1, ND))
    h00 = mu[1] + s * mu[0]
    h01 = mu[2] + s * mu[1]
    h02 = mu[3] + s * mu[2]
    h11 = h02
    h12 = mu[4] + s * mu[3]
    h22 = mu[5] + s * mu[4]
    l10, l20 = h01 / h00, h02 / h00
    d1 = h11 - l10 * h01
    e1 = h12 - l20 * h01
    l21 = e1 / d1
    d2 = h22 - l20 * h02 - l21 * e1
    y1 = mu[1] - l10 * mu[0]
    y2 = mu[2] - l20 * mu[0] - l21 * y1
    c2 = y2 / d2
    c1 = y1 / d1 - l21 * c2
    c0 = mu[0] / h00 - l10 * c1 - l20 * c2

    weights[...] = jnp.concatenate([c0, c1, c2] + [jnp.zeros((1, ND), F32)] * 5, axis=0)

    for i in range(len(pieces)):
        sent(i)
    for stage in range(2):
        for k in range(1, groups[stage][0]):
            group_copy(stage, k).wait_send()


def store_kernel(zt, p1t, p2t, weights, out_ref, xt, sem):
    rows = zt.shape[0]
    c0, c1, c2 = weights[0:1, :], weights[1:2, :], weights[2:3, :]

    def copy(r):
        return pltpu.make_async_copy(xt.at[r], out_ref.at[:, r, 0, :], sem.at[r])

    def combine(r, carry):
        xt[r] = c0 * zt[r] + c1 * p1t[r] + c2 * p2t[r]
        copy(r).start()
        return carry

    def finish(r, carry):
        copy(r).wait()
        return carry

    lax.fori_loop(0, rows, combine, 0)
    lax.fori_loop(0, rows, finish, 0)


def on_device(grid_rows, grid_cols, depth_rows, phase, pairs):
    m, rows, cols = phase.shape
    total_rows, total_cols = rows + 2 * HALO, cols + 2 * PAD
    y_len = grid_rows // depth_rows
    field = pltpu.VMEM((total_rows, total_cols, ND), F32)
    flat = pltpu.VMEM((rows, ND, cols), F32)
    dma = pltpu.SemaphoreType.DMA
    pieces = 6 + 2 * (rows // 8)
    parts = pl.pallas_call(
        lambda *refs: krylov_kernel(grid_rows, grid_cols, depth_rows, *refs),
        name="krylov",
        out_shape=[jax.ShapeDtypeStruct((rows, ND, cols), F32)] * 3 + [jax.ShapeDtypeStruct((8, ND), F32)],
        in_specs=[pl.BlockSpec(memory_space=pltpu.HBM)] * 2,
        out_specs=[pl.BlockSpec(memory_space=pltpu.VMEM)] * 4,
        scratch_shapes=[
            pltpu.VMEM((2, m), jnp.int32),
            pltpu.VMEM((rows, m, cols), F32),
            field, field, field, field, field,
            pltpu.VMEM((4 * ND, ND), BF16),
            pltpu.VMEM((8, 8, ND), F32),
            pltpu.VMEM((3, 1, ND), F32),
            pltpu.VMEM((y_len * grid_cols, 1, ND), F32),
            pltpu.VMEM((depth_rows, 1, ND), F32),
            pltpu.VMEM((cols + 2 * DIST_COL, ND), F32),
            dma, dma((rows,)),
            dma((pieces,)), dma((pieces,)),
            dma((y_len * grid_cols,)), dma((y_len * grid_cols,)),
            dma((depth_rows,)), dma((depth_rows,)),
        ],
        compiler_params=pltpu.CompilerParams(
            collective_id=0, has_side_effects=True, vmem_limit_bytes=40 * 1024 * 1024
        ),
    )(phase.reshape(m, rows, 1, cols), pltpu.with_memory_space_constraint(pairs.T, pltpu.HBM))
    out = pl.pallas_call(
        store_kernel,
        name="store",
        out_shape=jax.ShapeDtypeStruct((ND, rows, 1, cols), F32),
        in_specs=[pl.BlockSpec(memory_space=pltpu.VMEM)] * 4,
        out_specs=pl.BlockSpec(memory_space=pltpu.HBM),
        scratch_shapes=[flat, dma((rows,))],
        compiler_params=pltpu.CompilerParams(vmem_limit_bytes=16 * 1024 * 1024),
    )(*parts)
    return out.reshape(ND, rows, cols)


def solution(mesh, depth=8):
    grid_rows, grid_cols = mesh.shape["row"], mesh.shape["col"]

    def body(phase, pairs):
        return on_device(grid_rows, grid_cols, depth, phase, pairs)

    return jax.shard_map(
        body,
        mesh=mesh,
        in_specs=(P(None, "row", "col"), P()),
        out_specs=P(None, "row", "col"),
        check_vma=False,
    )
```

time: 55.8 us -> 35.1 us (0.63)
  Pallas kernels: 52.6 us -> 35 us
  local copies, waits for them, and re-layouts: 3.08 us -> 0 us
    pallas_call x1, Pallas kernels: 52.6 us -> 33.4 us  [on_device(): pl.pallas_call(lambda *refs: krylov_kernel(grid_rows, grid_cols, depth_ro...]
    unnamed x1 -> x0, local copies, waits for them, and re-layouts: 3.08 us -> none
    pallas_call x0 -> x1, Pallas kernels: none -> 1.59 us  [on_device(): pl.pallas_call(store_kernel, name='store', out_shape=jax.ShapeDtypeStruct...]
where the time goes in v1:
time: 35.1 us; the launch traced here: 35 us
  Pallas kernels  35 us (100%)
    pallas_call x1, Pallas kernels, on_device(): pl.pallas_call(lambda *refs: krylov_kernel(grid_rows, grid_cols, depth_ro...  33.4 us
    pallas_call x1, Pallas kernels, on_device(): pl.pallas_call(store_kernel, name='store', out_shape=jax.ShapeDtypeStruct...  1.59 us

profile of v1, /device:TPU:1, one launch (start us, length us, event | category | flops | bytes accessed | tf_op | source)
XLA Modules:
  0.0 35.0 jit_solution(16922703233854391190)
XLA Ops:
  0.0 33.4 %krylov.1 = (f32[32,128,128]{2,1,0:T(8,128)S(1)}, f32[32,128,128]{2,1,0:T(8,128)S(1)}, f32[32,128,128]{2,1,0:T(8,128)S(1)}, f32[8,128]{1,0:T(8,128)S(1)}) custom-call(f32[512,32,1,128]{3,2,1,0:T(1,128)} %bitcast.3, s32[2,512]{1,0:T(2,128)} %bitcast.4), custom_call_target="tpu_custom_call" | custom-call | tf_op jit(solution)/shard_map/krylov/pallas_call | solution.py:390
  33.4 1.6 %store.1 = f32[128,32,1,128]{3,2,1,0:T(1,128)} custom-call(f32[32,128,128]{2,1,0:T(8,128)S(1)} %get-tuple-element.9.zt, f32[32,128,128]{2,1,0:T(8,128)S(1)} %get-tuple-element.10.p1t, f32[32,128,128]{2,1,0:T(8,128)S(1)} %get-tuple-element.11.p2t, f32[8,128]{1,0:T(8,128)S(1)} %get-tuple-element.12.weights), custom_call_target="tpu_custom_call" | custom-call | tf_op jit(solution)/shard_map/store/pallas_call | solution.py:415

commit v2 on v1

--- a/solution.py
+++ b/solution.py
@@ -8,6 +8,7 @@
 ND = 128
 LAM2 = 0.8 * 0.8
 HALO = 5
+NEAR = 3
 PAD = 16
 DIST_COL = 8
 MESH = pl.DeviceIdType.MESH
@@ -26,11 +27,10 @@
 def krylov_kernel(
     grid_rows, grid_cols, depth_rows,
     phase_ref, pairs_hbm, zt, p1t, p2t, weights,
-    pairs_ref, ph, z, w1, q1, w2, q2, nmat, acc, tot, in1, in2, cmask,
+    pairs_ref, ph, z, w1, q1, w2, q2, nmat, acc, tot, in1, in2,
     pairs_sem, load_sem, halo_send, halo_recv, s1s, s1r, s2s, s2r,
 ):
     rows, cols = ph.shape[0], ph.shape[2]
-    wide = cols + 2 * DIST_COL
     row, col = lax.axis_index("row"), lax.axis_index("col")
     y_len = grid_rows // depth_rows
     row_y, row_z = row // depth_rows, lax.rem(row, depth_rows)
@@ -51,14 +51,10 @@
     def load(r):
         return pltpu.make_async_copy(phase_ref.at[:, r, 0, :], ph.at[r], load_sem.at[r])
 
+    top_rows, low_rows = range(0, HALO), range(rows - HALO, rows)
+    rest = [range(HALO, rows // 2), range(rows // 2, rows - HALO)]
     load_pairs = pltpu.make_async_copy(pairs_hbm, pairs_ref, pairs_sem)
     load_pairs.start()
-    strips = [0, rows - 8] + list(range(8, rows - 8, 8))
-    for r in range(4):
-        load(r).start()
-
-    lax.fori_loop(0, total_rows, clear_sides, 0)
-    lax.fori_loop(0, HALO, clear_ends, 0)
 
     around = [(-1, 0), (1, 0), (0, -1), (0, 1), (-1, -1), (-1, 1), (1, -1), (1, 1)]
 
@@ -86,18 +82,20 @@
         (depth_rows, z_peer, in2, s2s, s2r),
     ]
     barrier = pltpu.get_barrier_semaphore()
+    for size, peer, _buf, _s, _r in reversed(groups):
+        for k in range(1, size):
+            pl.semaphore_signal(barrier, inc=1, device_id=peer(k), device_id_type=MESH)
+    for part in [top_rows, low_rows] + rest:
+        for r in part:
+            load(r).start()
+    lax.fori_loop(0, total_rows, clear_sides, 0)
+    lax.fori_loop(0, HALO, clear_ends, 0)
     for dr, dc in around:
         @pl.when(exists(dr, dc))
         def _():
             pl.semaphore_signal(barrier, inc=1, device_id=(row + dr, col + dc), device_id_type=MESH)
-    for size, peer, _buf, _s, _r in groups:
-        for k in range(1, size):
-            pl.semaphore_signal(barrier, inc=1, device_id=peer(k), device_id_type=MESH)
 
     load_pairs.wait()
-    for base in strips:
-        for r in range(max(base, 4), base + 8):
-            load(r).start()
     dates = lax.broadcasted_iota(jnp.int32, (ND, pairs_ref.shape[1]), 0)
     later = (dates == pairs_ref[1:2, :]).astype(F32)
     earlier = (dates == pairs_ref[0:1, :]).astype(F32)
@@ -114,45 +112,47 @@
     n_lo = (shifted - n_hi.astype(F32)).astype(BF16)
     nmat[...] = jnp.concatenate([n_hi, n_hi, n_hi, n_lo], axis=0)
 
-    side = lax.broadcasted_iota(jnp.int32, (wide, ND), 0)
     left_ok = jnp.where(col > 0, 1.0, 0.0)
     right_ok = jnp.where(col < grid_cols - 1, 1.0, 0.0)
-    cmask[...] = jnp.where(
-        side < DIST_COL, left_ok, jnp.where(side >= DIST_COL + cols, right_ok, 1.0)
-    )
     top_ok = jnp.where(row > 0, 1.0, 0.0)
     bottom_ok = jnp.where(row < grid_rows - 1, 1.0, 0.0)
-    def make_z(r):
-        parts = []
-        for j in range(8):
-            load(r + j).wait()
-            parts.append(split(ph[r + j], 2))
-        for half in (parts[:4], parts[4:]):
+    def make_z(part, group):
+        part = list(part)
+        for r in part:
+            load(r).wait()
+        for some in [part[i:i + group] for i in range(0, len(part), group)]:
+            terms = [split(ph[r], 2) for r in some]
             field = sum(
-                jnp.dot(gt, jnp.concatenate([p[t] for p in half], axis=1), preferred_element_type=F32)
+                jnp.dot(gt, jnp.concatenate([x[t] for x in terms], axis=1), preferred_element_type=F32)
                 for t in range(2)
             )
-            for j in range(4):
-                part = field[:, j * cols:(j + 1) * cols]
-                zt[r + j] = part
-                z[HALO + r + j, first:last, :] = part.T
-            r = r + 4
-
-    top, low = HALO, rows
-    pieces = [(-1, 0, top, HALO + rows, HALO), (1, 0, low, 0, HALO)]
-    for dc in (-1, 1):
-        pieces += [(-1, dc, top, HALO + rows, HALO - 1), (1, dc, low + 1, 1, HALO - 1)]
-    for r in strips:
-        pieces += [(0, dc, HALO + r, HALO + r, 8) for dc in (-1, 1)]
-    edge_c = {-1: first, 1: last - DIST_COL, 0: first}
-    size_c = {-1: DIST_COL, 1: DIST_COL, 0: cols}
-    land_c = {-1: last, 1: first - DIST_COL, 0: first}
+            for j, r in enumerate(some):
+                one = field[:, j * cols:(j + 1) * cols]
+                zt[r] = one
+                z[HALO + r, first:last, :] = one.T
+
+    far = HALO - NEAR
+    top, low, end = HALO, rows + HALO, HALO + rows
+    half = rows // 2
+    pieces = []
+    for dr, source, target in ((-1, top, end), (1, low - NEAR, HALO - NEAR)):
+        pieces.append((dr, 0, source, target, NEAR))
+        source, target = (top, end) if dr < 0 else (low - HALO + 1, 1)
+        pieces += [(dr, dc, source, target, HALO - 1) for dc in (-1, 1)]
+        source, target = (top + NEAR, end + NEAR) if dr < 0 else (low - HALO, 0)
+        pieces.append((dr, 0, source, target, far))
+    for r in (0, half):
+        pieces += [(0, dc, HALO + r, HALO + r, half) for dc in (-1, 1)]
+    near_pieces, far_pieces, side_pieces = (0, 1, 2, 4, 5, 6), (3, 7), (8, 9, 10, 11)
 
     def halo(i):
         dr, dc, source, target, count = pieces[i]
+        width = cols if dc == 0 else HALO - 1 if dr else DIST_COL
+        source_col = last - width if dc == 1 else first
+        target_col = {-1: last, 0: first, 1: first - width}[dc]
         return pltpu.make_async_remote_copy(
-            src_ref=z.at[pl.ds(source, count), pl.ds(edge_c[dc], size_c[dc]), :],
-            dst_ref=z.at[pl.ds(target, count), pl.ds(land_c[dc], size_c[dc]), :],
+            src_ref=z.at[pl.ds(source, count), pl.ds(source_col, width), :],
+            dst_ref=z.at[pl.ds(target, count), pl.ds(target_col, width), :],
             send_sem=halo_send.at[i],
             recv_sem=halo_recv.at[i],
             device_id=(row + dr, col + dc),
@@ -175,61 +175,69 @@
         def _():
             halo(i).wait_send()
 
-    for r in strips[:2]:
-        make_z(r)
+    make_z(top_rows, 5)
+    make_z(low_rows, 5)
+    make_z(rest[0], 4)
     n_peers = sum(size - 1 for size, *_ in groups)
     n_around = jnp.int32(0)
     for dr, dc in around:
         n_around = n_around + jnp.where(exists(dr, dc), 1, 0)
     pl.semaphore_wait(barrier, n_around + n_peers)
-    for i in range(10):
+    for i in (0, 4, 1, 2, 5, 6, 3, 7) + side_pieces[:2]:
         send(i)
-    for part, r in enumerate(strips[2:]):
-        make_z(r)
-        for i in (10 + 2 * part, 11 + 2 * part):
-            send(i)
+    make_z(rest[1], 4)
+    for i in side_pieces[2:]:
+        send(i)
 
     acc[...] = jnp.zeros_like(acc)
-    work = pl.ds(PAD - DIST_COL, wide)
-    before = pl.ds(PAD - DIST_COL - 1, wide)
-    after = pl.ds(PAD - DIST_COL + 1, wide)
-
-    def lap(buf, e):
-        beside = buf[e - 1, work, :] + buf[e + 1, work, :] + buf[e, before, :] + buf[e, after, :]
-        return 4.0 * buf[e, work, :] - beside
+
+    everything = [(first - DIST_COL, cols + 2 * DIST_COL)]
+    own_columns = [(first, cols)]
+    inner = [[(first + edge, cols - 2 * edge)] for edge in (8, 16)]
+    outer = [[(first - DIST_COL, DIST_COL + edge), (last - edge, DIST_COL + edge)] for edge in (8, 16)]
+
+    def lap(buf, e, span):
+        at, width = span
+        here = pl.ds(at, width)
+        beside = buf[e - 1, here, :] + buf[e + 1, here, :] + buf[e, pl.ds(at - 1, width), :] + buf[e, pl.ds(at + 1, width), :]
+        return 4.0 * buf[e, here, :] - beside
 
     def normal_times(values):
-        pieces = []
-        for value in values:
-            hi, mid, lo = split(value, 3)
-            pieces.append(jnp.concatenate([hi, mid, lo, hi], axis=1))
-        height = values[0].shape[0]
+        def times(some):
+            pieces = []
+            for value in some:
+                hi, mid, lo = split(value, 3)
+                pieces.append(jnp.concatenate([hi, mid, lo, hi], axis=1))
+            both = jnp.dot(jnp.concatenate(pieces, axis=0), nmat[...], preferred_element_type=F32)
+            products, at = [], 0
+            for value in some:
+                products.append(both[at:at + value.shape[0], :])
+                at += value.shape[0]
+            return products
+
         half = (len(values) + 1) // 2
-        products = []
-        for some in (pieces[:half], pieces[half:]):
-            both = jnp.dot(jnp.concatenate(some, axis=0), nmat[...], preferred_element_type=F32)
-            products += [both[i * height:(i + 1) * height, :] for i in range(len(some))]
-        return products
-
-    def own(value):
-        return value[DIST_COL:DIST_COL + cols, :]
+        return times(values[:half]) + times(values[half:])
+
+    def own(value, span):
+        lo = max(first - span[0], 0)
+        return value[lo:lo + min(span[0] + span[1], last) - max(span[0], first), :]
 
     def folded(value):
-        return jnp.sum(value.reshape(cols // 8, 8, ND), axis=0)
-
-    def masked(value, scale):
-        if scale is None:
-            ends = (value[:DIST_COL] * cmask[:DIST_COL], value[-DIST_COL:] * cmask[-DIST_COL:])
-            return jnp.concatenate([ends[0], own(value), ends[1]], axis=0)
-        return value * (cmask[...] * scale)
+        return jnp.sum(value.reshape(value.shape[0] // 8, 8, ND), axis=0)
+
+    def masked(value, span, scale):
+        lo, hi = first - span[0], last - span[0]
+        parts = [own(value, span)]
+        if lo > 0:
+            parts = [value[:lo] * left_ok] + parts
+        if span[1] > hi:
+            parts = parts + [value[hi:] * right_ok]
+        value = jnp.concatenate(parts, axis=0) if len(parts) > 1 else parts[0]
+        return value if scale is None else value * scale
 
     def blocks(lo, hi, block, body):
-        if hi - lo == block:
-            body(lo)
-            return
-
         def step(i, carry):
-            body(lo + block * i)
+            body([lo + block * i + j for j in range(block)])
             return carry
         lax.fori_loop(0, (hi - lo) // block, step, 0)
 
@@ -241,65 +249,77 @@
     def counts(e):
         return not isinstance(e, int) or HALO <= e < HALO + rows
 
-    def lap_rows(src, dst, lo, hi, block):
-        def body(base):
-            for e in [base + i for i in range(block)]:
-                dst[e, work, :] = masked(lap(src, e), scale_of(e))
-        blocks(lo, hi, block, body)
-
-    def k_rows(src, lap_buf, dst, flat, lo, hi, block, moment):
-        def body(base):
-            es = [base + i for i in range(block)]
-            sums = [jnp.zeros((8, ND), F32)] * 3
-            products = normal_times([src[e, work, :] for e in es])
-            for e, product in zip(es, products):
-                value = src[e, work, :]
-                result = masked(product + LAM2 * lap(lap_buf, e), scale_of(e))
-                dst[e, work, :] = result
-                if counts(e):
-                    mine, new = own(value), own(result)
-                    flat[e - HALO] = new.T
-                    if moment == 1:
-                        sums[0] = sums[0] + folded(mine * mine)
-                    sums[1] = sums[1] + folded(mine * new)
-                    sums[2] = sums[2] + folded(new * new)
-            if moment == 1:
-                acc[0] += sums[0]
-            acc[moment] += sums[1]
-            acc[moment + 1] += sums[2]
-        blocks(lo, hi, block, body)
-
-    def last_rows(lo, hi, block):
-        def body(base):
-            es = [base + i for i in range(block)]
-            products = normal_times([q2[e, first:last, :] for e in es])
-            total = jnp.zeros((8, ND), F32)
-            for e, product in zip(es, products):
-                bent = own(lap(q2, e))
-                total = total + folded(q2[e, first:last, :] * product + LAM2 * (bent * bent))
-            acc[5] += total
-        blocks(lo, hi, block, body)
-
-    for i in range(6, len(pieces)):
+    def lap_rows(src, dst, spans, es):
+        for e in es:
+            for span in spans:
+                dst[e, pl.ds(*span), :] = masked(lap(src, e, span), span, scale_of(e))
+
+    def k_rows(src, lap_buf, dst, flat, moment, spans, es):
+        sums = [jnp.zeros((8, ND), F32)] * 3
+        places = [(e, span) for e in es for span in spans]
+        products = normal_times([src[e, pl.ds(*span), :] for e, span in places])
+        for (e, span), product in zip(places, products):
+            value = src[e, pl.ds(*span), :]
+            result = masked(product + LAM2 * lap(lap_buf, e, span), span, scale_of(e))
+            dst[e, pl.ds(*span), :] = result
+            if counts(e):
+                mine, new = own(value, span), own(result, span)
+                if flat is not None:
+                    flat[e - HALO] = mine.T
+                if moment == 1:
+                    sums[0] = sums[0] + folded(mine * mine)
+                sums[1] = sums[1] + folded(mine * new)
+                sums[2] = sums[2] + folded(new * new)
+        if moment == 1:
+            acc[0] += sums[0]
+        acc[moment] += sums[1]
+        acc[moment + 1] += sums[2]
+
+    def last_rows(spans, es):
+        (span,) = spans
+        products = normal_times([q2[e, pl.ds(*span), :] for e in es])
+        total = jnp.zeros((8, ND), F32)
+        for e, product in zip(es, products):
+            value, bent = q2[e, pl.ds(*span), :], lap(q2, e, span)
+            p2t[e - HALO] = value.T
+            total = total + folded(value * product + LAM2 * (bent * bent))
+        acc[5] += total
+
+    stages = [
+        lambda spans, es: lap_rows(z, w1, spans, es),
+        lambda spans, es: k_rows(z, w1, q1, None, 1, spans, es),
+        lambda spans, es: lap_rows(q1, w2, spans, es),
+        lambda spans, es: k_rows(q1, w2, q2, p1t, 3, spans, es),
+        last_rows,
+    ]
+    last_stage = len(stages)
+    spans_of = [everything] * (last_stage - 1) + [own_columns]
+
+    def middle(k, spans, block):
+        blocks(HALO + k, HALO + rows - k, block, lambda es: stages[k - 1](spans, es))
+
+    middle(1, inner[0], 3)
+    middle(2, inner[1], 14)
+    for i in side_pieces:
         arrived(i)
-    lap_rows(z, w1, 6, 36, 3)
-    k_rows(z, w1, q1, p1t, 7, 35, 7, 1)
-    lap_rows(q1, w2, 8, 34, 2)
-    k_rows(q1, w2, q2, p2t, 9, 33, 8, 3)
-    last_rows(10, 32, 11)
-
-    for i in range(6):
+    middle(1, outer[0], 6)
+    middle(2, outer[1], 14)
+    middle(3, everything, 2)
+    middle(4, everything, 12)
+    middle(5, own_columns, 11)
+
+    def ends(done, ready):
+        for k, stage in enumerate(stages, 1):
+            above = range(HALO - ready + k, HALO - done + k)
+            below = range(HALO + rows + done - k, HALO + rows + ready - k)
+            stage(spans_of[k - 1], list(above) + list(below))
+
+    for i in near_pieces:
         arrived(i)
-    for lo in (1, 36):
-        lap_rows(z, w1, lo, lo + 5, 5)
-    for lo in (2, 35):
-        k_rows(z, w1, q1, p1t, lo, lo + 5, 5, 1)
-    for lo in (3, 34):
-        lap_rows(q1, w2, lo, lo + 5, 5)
-    for lo in (4, 33):
-        k_rows(q1, w2, q2, p2t, lo, lo + 5, 5, 3)
-    for lo in (5, 32):
-        last_rows(lo, lo + 5, 5)
+    ends(0, NEAR)
+    for i in far_pieces:
+        arrived(i)
+    ends(NEAR, HALO)
 
     lines = jnp.concatenate([jnp.sum(acc[j], axis=0, keepdims=True) for j in range(8)], axis=0)
     lines = jnp.broadcast_to(jnp.sum(lines, axis=1, keepdims=True), (8, ND))
@@ -386,7 +406,7 @@
     field = pltpu.VMEM((total_rows, total_cols, ND), F32)
     flat = pltpu.VMEM((rows, ND, cols), F32)
     dma = pltpu.SemaphoreType.DMA
-    pieces = 6 + 2 * (rows // 8)
+    pieces = 12
     parts = pl.pallas_call(
         lambda *refs: krylov_kernel(grid_rows, grid_cols, depth_rows, *refs),
         name="krylov",
@@ -402,7 +422,6 @@
             pltpu.VMEM((3, 1, ND), F32),
             pltpu.VMEM((y_len * grid_cols, 1, ND), F32),
             pltpu.VMEM((depth_rows, 1, ND), F32),
-            pltpu.VMEM((cols + 2 * DIST_COL, ND), F32),
             dma, dma((rows,)),
             dma((pieces,)), dma((pieces,)),
             dma((y_len * grid_cols,)), dma((y_len * grid_cols,)),

time: 35.1 us -> 33.1 us (0.943)
  Pallas kernels: 35 us -> 33 us
    pallas_call x1, Pallas kernels: 33.4 us -> 31.4 us  [on_device(): pl.pallas_call(lambda *refs: krylov_kernel(grid_rows, grid_cols, depth_ro...]
where the time goes in v2:
time: 33.1 us; the launch traced here: 33 us
  Pallas kernels  33 us (100%)
    pallas_call x1, Pallas kernels, on_device(): pl.pallas_call(lambda *refs: krylov_kernel(grid_rows, grid_cols, depth_ro...  31.4 us
    pallas_call x1, Pallas kernels, on_device(): pl.pallas_call(store_kernel, name='store', out_shape=jax.ShapeDtypeStruct...  1.59 us

profile of v2, /device:TPU:1, one launch (start us, length us, event | category | flops | bytes accessed | tf_op | source)
XLA Modules:
  0.0 33.0 jit_solution(16817003193476772437)
XLA Ops:
  0.0 31.4 %krylov.1 = (f32[32,128,128]{2,1,0:T(8,128)S(1)}, f32[32,128,128]{2,1,0:T(8,128)S(1)}, f32[32,128,128]{2,1,0:T(8,128)S(1)}, f32[8,128]{1,0:T(8,128)S(1)}) custom-call(f32[512,32,1,128]{3,2,1,0:T(1,128)} %bitcast.3, s32[2,512]{1,0:T(2,128)} %bitcast.4), custom_call_target="tpu_custom_call" | custom-call | tf_op jit(solution)/shard_map/krylov/pallas_call | solution.py:410
  31.4 1.6 %store.1 = f32[128,32,1,128]{3,2,1,0:T(1,128)} custom-call(f32[32,128,128]{2,1,0:T(8,128)S(1)} %get-tuple-element.9.zt, f32[32,128,128]{2,1,0:T(8,128)S(1)} %get-tuple-element.10.p1t, f32[32,128,128]{2,1,0:T(8,128)S(1)} %get-tuple-element.11.p2t, f32[8,128]{1,0:T(8,128)S(1)} %get-tuple-element.12.weights), custom_call_target="tpu_custom_call" | custom-call | tf_op jit(solution)/shard_map/store/pallas_call | solution.py:434

commit v3 on v2

--- a/solution.py
+++ b/solution.py
@@ -147,7 +147,7 @@
 
     def halo(i):
         dr, dc, source, target, count = pieces[i]
-        width = cols if dc == 0 else HALO - 1 if dr else DIST_COL
+        width = cols if dc == 0 else HALO - 1 if dr else HALO
         source_col = last - width if dc == 1 else first
         target_col = {-1: last, 0: first, 1: first - width}[dc]
         return pltpu.make_async_remote_copy(
@@ -177,24 +177,24 @@
 
     make_z(top_rows, 5)
     make_z(low_rows, 5)
-    make_z(rest[0], 4)
     n_peers = sum(size - 1 for size, *_ in groups)
     n_around = jnp.int32(0)
     for dr, dc in around:
         n_around = n_around + jnp.where(exists(dr, dc), 1, 0)
     pl.semaphore_wait(barrier, n_around + n_peers)
-    for i in (0, 4, 1, 2, 5, 6, 3, 7) + side_pieces[:2]:
+    for i in (0, 4, 1, 2, 5, 6, 3, 7):
         send(i)
-    make_z(rest[1], 4)
-    for i in side_pieces[2:]:
-        send(i)
+    for part, side in zip(rest, (side_pieces[:2], side_pieces[2:])):
+        make_z(part, 4)
+        for i in side:
+            send(i)
 
     acc[...] = jnp.zeros_like(acc)
 
     everything = [(first - DIST_COL, cols + 2 * DIST_COL)]
     own_columns = [(first, cols)]
-    inner = [[(first + edge, cols - 2 * edge)] for edge in (8, 16)]
-    outer = [[(first - DIST_COL, DIST_COL + edge), (last - edge, DIST_COL + edge)] for edge in (8, 16)]
+    inner = [[(first + edge, cols - 2 * edge)] for edge in (8, 16, 24, 32)]
+    outer = [[(first - DIST_COL, DIST_COL + edge), (last - edge, DIST_COL + edge)] for edge in (8, 16, 24, 32)]
 
     def lap(buf, e, span):
         at, width = span
@@ -254,7 +254,7 @@
             for span in spans:
                 dst[e, pl.ds(*span), :] = masked(lap(src, e, span), span, scale_of(e))
 
-    def k_rows(src, lap_buf, dst, flat, moment, spans, es):
+    def k_rows(src, lap_buf, dst, moment, spans, es):
         sums = [jnp.zeros((8, ND), F32)] * 3
         places = [(e, span) for e in es for span in spans]
         products = normal_times([src[e, pl.ds(*span), :] for e, span in places])
@@ -264,8 +264,6 @@
             dst[e, pl.ds(*span), :] = result
             if counts(e):
                 mine, new = own(value, span), own(result, span)
-                if flat is not None:
-                    flat[e - HALO] = mine.T
                 if moment == 1:
                     sums[0] = sums[0] + folded(mine * mine)
                 sums[1] = sums[1] + folded(mine * new)
@@ -281,15 +279,16 @@
         total = jnp.zeros((8, ND), F32)
         for e, product in zip(es, products):
             value, bent = q2[e, pl.ds(*span), :], lap(q2, e, span)
+            p1t[e - HALO] = q1[e, first:last, :].T
             p2t[e - HALO] = value.T
             total = total + folded(value * product + LAM2 * (bent * bent))
         acc[5] += total
 
     stages = [
         lambda spans, es: lap_rows(z, w1, spans, es),
-        lambda spans, es: k_rows(z, w1, q1, None, 1, spans, es),
+        lambda spans, es: k_rows(z, w1, q1, 1, spans, es),
         lambda spans, es: lap_rows(q1, w2, spans, es),
-        lambda spans, es: k_rows(q1, w2, q2, p1t, 3, spans, es),
+        lambda spans, es: k_rows(q1, w2, q2, 3, spans, es),
         last_rows,
     ]
     last_stage = len(stages)
@@ -298,14 +297,12 @@
     def middle(k, spans, block):
         blocks(HALO + k, HALO + rows - k, block, lambda es: stages[k - 1](spans, es))
 
-    middle(1, inner[0], 3)
-    middle(2, inner[1], 14)
+    for k, block in enumerate((3, 14, 2, 12), 1):
+        middle(k, inner[k - 1], block)
     for i in side_pieces:
         arrived(i)
-    middle(1, outer[0], 6)
-    middle(2, outer[1], 14)
-    middle(3, everything, 2)
-    middle(4, everything, 12)
+    for k, block in enumerate((6, 14, 2, 12), 1):
+        middle(k, outer[k - 1], block)
     middle(5, own_columns, 11)
 
     def ends(done, ready):

time: 33.1 us -> 32.9 us (level)
  no operation moved by 1% of the time
where the time goes in v3:
time: 32.9 us; the launch traced here: 32.8 us
  Pallas kernels  32.8 us (100%)
    pallas_call x1, Pallas kernels, on_device(): pl.pallas_call(lambda *refs: krylov_kernel(grid_rows, grid_cols, depth_ro...  31.2 us
    pallas_call x1, Pallas kernels, on_device(): pl.pallas_call(store_kernel, name='store', out_shape=jax.ShapeDtypeStruct...  1.59 us

profile of v3, /device:TPU:1, one launch (start us, length us, event | category | flops | bytes accessed | tf_op | source)
XLA Modules:
  0.0 32.8 jit_solution(14889902951170505493)
XLA Ops:
  0.0 31.2 %krylov.1 = (f32[32,128,128]{2,1,0:T(8,128)S(1)}, f32[32,128,128]{2,1,0:T(8,128)S(1)}, f32[32,128,128]{2,1,0:T(8,128)S(1)}, f32[8,128]{1,0:T(8,128)S(1)}) custom-call(f32[512,32,1,128]{3,2,1,0:T(1,128)} %bitcast.3, s32[2,512]{1,0:T(2,128)} %bitcast.4), custom_call_target="tpu_custom_call" | custom-call | tf_op jit(solution)/shard_map/krylov/pallas_call | solution.py:407
  31.2 1.6 %store.1 = f32[128,32,1,128]{3,2,1,0:T(1,128)} custom-call(f32[32,128,128]{2,1,0:T(8,128)S(1)} %get-tuple-element.9.zt, f32[32,128,128]{2,1,0:T(8,128)S(1)} %get-tuple-element.10.p1t, f32[32,128,128]{2,1,0:T(8,128)S(1)} %get-tuple-element.11.p2t, f32[8,128]{1,0:T(8,128)S(1)} %get-tuple-element.12.weights), custom_call_target="tpu_custom_call" | custom-call | tf_op jit(solution)/shard_map/store/pallas_call | solution.py:431

commit v4 on v3

--- a/solution.py
+++ b/solution.py
@@ -48,13 +48,19 @@
             z[base + e, first:last, :] = jnp.zeros((cols, ND), F32)
         return carry
 
-    def load(r):
-        return pltpu.make_async_copy(phase_ref.at[:, r, 0, :], ph.at[r], load_sem.at[r])
+    def load(i, r):
+        return pltpu.make_async_copy(phase_ref.at[:, r, 0, :], ph.at[r], load_sem.at[i])
+
+    def loaded(i):
+        here = ph.at[pl.ds(parts[i].start, len(parts[i]))]
+        pltpu.make_async_copy(here, here, load_sem.at[i]).wait()
 
     top_rows, low_rows = range(0, HALO), range(rows - HALO, rows)
-    rest = [range(HALO, rows // 2), range(rows // 2, rows - HALO)]
+    parts = [top_rows, low_rows, range(HALO, rows // 2), range(rows // 2, rows - HALO)]
     load_pairs = pltpu.make_async_copy(pairs_hbm, pairs_ref, pairs_sem)
     load_pairs.start()
+    for r in top_rows:
+        load(0, r).start()
 
     around = [(-1, 0), (1, 0), (0, -1), (0, 1), (-1, -1), (-1, 1), (1, -1), (1, 1)]
 
@@ -85,9 +91,9 @@
     for size, peer, _buf, _s, _r in reversed(groups):
         for k in range(1, size):
             pl.semaphore_signal(barrier, inc=1, device_id=peer(k), device_id_type=MESH)
-    for part in [top_rows, low_rows] + rest:
-        for r in part:
-            load(r).start()
+    for i in (1, 2, 3):
+        for r in parts[i]:
+            load(i, r).start()
     lax.fori_loop(0, total_rows, clear_sides, 0)
     lax.fori_loop(0, HALO, clear_ends, 0)
     for dr, dc in around:
@@ -116,11 +122,10 @@
     right_ok = jnp.where(col < grid_cols - 1, 1.0, 0.0)
     top_ok = jnp.where(row > 0, 1.0, 0.0)
     bottom_ok = jnp.where(row < grid_rows - 1, 1.0, 0.0)
-    def make_z(part, group):
-        part = list(part)
-        for r in part:
-            load(r).wait()
-        for some in [part[i:i + group] for i in range(0, len(part), group)]:
+    def make_z(i, group):
+        part = list(parts[i])
+        loaded(i)
+        for some in [part[at:at + group] for at in range(0, len(part), group)]:
             terms = [split(ph[r], 2) for r in some]
             field = sum(
                 jnp.dot(gt, jnp.concatenate([x[t] for x in terms], axis=1), preferred_element_type=F32)
@@ -175,8 +180,8 @@
         def _():
             halo(i).wait_send()
 
-    make_z(top_rows, 5)
-    make_z(low_rows, 5)
+    make_z(0, 5)
+    make_z(1, 5)
     n_peers = sum(size - 1 for size, *_ in groups)
     n_around = jnp.int32(0)
     for dr, dc in around:
@@ -184,7 +189,7 @@
     pl.semaphore_wait(barrier, n_around + n_peers)
     for i in (0, 4, 1, 2, 5, 6, 3, 7):
         send(i)
-    for part, side in zip(rest, (side_pieces[:2], side_pieces[2:])):
+    for part, side in ((2, side_pieces[:2]), (3, side_pieces[2:])):
         make_z(part, 4)
         for i in side:
             send(i)
@@ -328,18 +333,28 @@
         return pltpu.make_async_remote_copy(
             src_ref=tot.at[stage],
             dst_ref=buf.at[k],
-            send_sem=s_sem.at[k],
-            recv_sem=r_sem.at[k],
+            send_sem=s_sem,
+            recv_sem=r_sem,
             device_id=peer(k),
             device_id_type=MESH,
+        )
+
+    def all_copies(stage):
+        size, peer, buf, s_sem, r_sem = groups[stage]
+        others = buf.at[pl.ds(1, size - 1)]
+        return pltpu.make_async_remote_copy(
+            src_ref=others, dst_ref=others, send_sem=s_sem, recv_sem=r_sem, device_id=peer(1), device_id_type=MESH
         )
 
     for stage in range(2):
         size = groups[stage][0]
         for k in range(1, size):
             group_copy(stage, k).start()
-        for k in range(1, size):
-            group_copy(stage, k).wait_recv()
+        if stage == 0:
+            for i in range(len(pieces)):
+                sent(i)
+        all_copies(stage).wait_send()
+        all_copies(stage).wait_recv()
         part = tot[stage]
         for k in range(1, size):
             part = part + groups[stage][2][k]
@@ -369,31 +384,21 @@
 
     weights[...] = jnp.concatenate([c0, c1, c2] + [jnp.zeros((1, ND), F32)] * 5, axis=0)
 
-    for i in range(len(pieces)):
-        sent(i)
-    for stage in range(2):
-        for k in range(1, groups[stage][0]):
-            group_copy(stage, k).wait_send()
-
 
 def store_kernel(zt, p1t, p2t, weights, out_ref, xt, sem):
     rows = zt.shape[0]
     c0, c1, c2 = weights[0:1, :], weights[1:2, :], weights[2:3, :]
 
     def copy(r):
-        return pltpu.make_async_copy(xt.at[r], out_ref.at[:, r, 0, :], sem.at[r])
+        return pltpu.make_async_copy(xt.at[r], out_ref.at[:, r, 0, :], sem)
 
     def combine(r, carry):
         xt[r] = c0 * zt[r] + c1 * p1t[r] + c2 * p2t[r]
         copy(r).start()
         return carry
 
-    def finish(r, carry):
-        copy(r).wait()
-        return carry
-
     lax.fori_loop(0, rows, combine, 0)
-    lax.fori_loop(0, rows, finish, 0)
+    pltpu.make_async_copy(xt, xt, sem).wait()
 
 
 def on_device(grid_rows, grid_cols, depth_rows, phase, pairs):
@@ -419,10 +424,9 @@
             pltpu.VMEM((3, 1, ND), F32),
             pltpu.VMEM((y_len * grid_cols, 1, ND), F32),
             pltpu.VMEM((depth_rows, 1, ND), F32),
-            dma, dma((rows,)),
+            dma, dma((4,)),
             dma((pieces,)), dma((pieces,)),
-            dma((y_len * grid_cols,)), dma((y_len * grid_cols,)),
-            dma((depth_rows,)), dma((depth_rows,)),
+            dma, dma, dma, dma,
         ],
         compiler_params=pltpu.CompilerParams(
             collective_id=0, has_side_effects=True, vmem_limit_bytes=40 * 1024 * 1024
@@ -434,7 +438,7 @@
         out_shape=jax.ShapeDtypeStruct((ND, rows, 1, cols), F32),
         in_specs=[pl.BlockSpec(memory_space=pltpu.VMEM)] * 4,
         out_specs=pl.BlockSpec(memory_space=pltpu.HBM),
-        scratch_shapes=[flat, dma((rows,))],
+        scratch_shapes=[flat, dma],
         compiler_params=pltpu.CompilerParams(vmem_limit_bytes=16 * 1024 * 1024),
     )(*parts)
     return out.reshape(ND, rows, cols)

time: 32.9 us -> 31.6 us (0.960)
  Pallas kernels: 32.8 us -> 31.5 us
    pallas_call x1, Pallas kernels: 31.2 us -> 30.2 us  [on_device(): pl.pallas_call(lambda *refs: krylov_kernel(grid_rows, grid_cols, depth_ro...]
where the time goes in v4:
time: 31.6 us; the launch traced here: 31.5 us
  Pallas kernels  31.5 us (100%)
    pallas_call x1, Pallas kernels, on_device(): pl.pallas_call(lambda *refs: krylov_kernel(grid_rows, grid_cols, depth_ro...  30.2 us
    pallas_call x1, Pallas kernels, on_device(): pl.pallas_call(store_kernel, name='store', out_shape=jax.ShapeDtypeStruct...  1.31 us

profile of v4, /device:TPU:1, one launch (start us, length us, event | category | flops | bytes accessed | tf_op | source)
XLA Modules:
  0.0 31.5 jit_solution(6160234946688379989)
XLA Ops:
  0.0 30.2 %krylov.1 = (f32[32,128,128]{2,1,0:T(8,128)S(1)}, f32[32,128,128]{2,1,0:T(8,128)S(1)}, f32[32,128,128]{2,1,0:T(8,128)S(1)}, f32[8,128]{1,0:T(8,128)S(1)}) custom-call(f32[512,32,1,128]{3,2,1,0:T(1,128)} %bitcast.3, s32[2,512]{1,0:T(2,128)} %bitcast.4), custom_call_target="tpu_custom_call" | custom-call | tf_op jit(solution)/shard_map/krylov/pallas_call | solution.py:412
  30.2 1.3 %store.1 = f32[128,32,1,128]{3,2,1,0:T(1,128)} custom-call(f32[32,128,128]{2,1,0:T(8,128)S(1)} %get-tuple-element.9.zt, f32[32,128,128]{2,1,0:T(8,128)S(1)} %get-tuple-element.10.p1t, f32[32,128,128]{2,1,0:T(8,128)S(1)} %get-tuple-element.11.p2t, f32[8,128]{1,0:T(8,128)S(1)} %get-tuple-element.12.weights), custom_call_target="tpu_custom_call" | custom-call | tf_op jit(solution)/shard_map/store/pallas_call | solution.py:435

commit v5 on v4

--- a/solution.py
+++ b/solution.py
@@ -306,9 +306,9 @@
         middle(k, inner[k - 1], block)
     for i in side_pieces:
         arrived(i)
-    for k, block in enumerate((6, 14, 2, 12), 1):
+    for k, block in enumerate((6, 28, 2, 24), 1):
         middle(k, outer[k - 1], block)
-    middle(5, own_columns, 11)
+    middle(5, own_columns, 22)
 
     def ends(done, ready):
         for k, stage in enumerate(stages, 1):

time: 31.6 us -> 31.6 us (level)
  no operation moved by 1% of the time
where the time goes in v5:
time: 31.6 us; the launch traced here: 31.5 us
  Pallas kernels  31.5 us (100%)
    pallas_call x1, Pallas kernels, on_device(): pl.pallas_call(lambda *refs: krylov_kernel(grid_rows, grid_cols, depth_ro...  30.2 us
    pallas_call x1, Pallas kernels, on_device(): pl.pallas_call(store_kernel, name='store', out_shape=jax.ShapeDtypeStruct...  1.31 us

profile of v5, /device:TPU:1, one launch (start us, length us, event | category | flops | bytes accessed | tf_op | source)
XLA Modules:
  0.0 31.5 jit_solution(17038358625172320628)
XLA Ops:
  0.0 30.2 %krylov.1 = (f32[32,128,128]{2,1,0:T(8,128)S(1)}, f32[32,128,128]{2,1,0:T(8,128)S(1)}, f32[32,128,128]{2,1,0:T(8,128)S(1)}, f32[8,128]{1,0:T(8,128)S(1)}) custom-call(f32[512,32,1,128]{3,2,1,0:T(1,128)} %bitcast.3, s32[2,512]{1,0:T(2,128)} %bitcast.4), custom_call_target="tpu_custom_call" | custom-call | tf_op jit(solution)/shard_map/krylov/pallas_call | solution.py:412
  30.2 1.3 %store.1 = f32[128,32,1,128]{3,2,1,0:T(1,128)} custom-call(f32[32,128,128]{2,1,0:T(8,128)S(1)} %get-tuple-element.9.zt, f32[32,128,128]{2,1,0:T(8,128)S(1)} %get-tuple-element.10.p1t, f32[32,128,128]{2,1,0:T(8,128)S(1)} %get-tuple-element.11.p2t, f32[8,128]{1,0:T(8,128)S(1)} %get-tuple-element.12.weights), custom_call_target="tpu_custom_call" | custom-call | tf_op jit(solution)/shard_map/store/pallas_call | solution.py:435
